TPU v7x, 32 devices: a whole 2x2x4 slice. The times are simulated.
32 devices in a mesh: rep: 4 (over z), tm: 4 (over x, core), space: 2 (over y).
Axes of the slice: x: 2, y: 2, z: 4, core: 2. Of those that a mesh axis runs over, the one named last changes fastest.
Arguments:
- spins: float32 [20, 3, 64, 4096], P('rep', None, 'tm', 'space'), may hold values from -4 to 4
- bond_right: float32 [4096], P('space'), may hold values from -4 to 4
- bond_down: float32 [4096], P('space'), may hold values from -4 to 4
- betas: float32 [20], P('rep'), may hold values from 0.2 to 2
- time_coupling: float32 [20], P('rep'), may hold values from 0.1 to 1
- thresholds: int32 [2, 20, 64, 4096], P(None, 'rep', 'tm', 'space'), may hold values from 0 to 8191
- partner: int32 [20], P('rep'), may hold values from 0 to 19, as said below
- accept: int32 [20], P('rep'), may hold values from 0 to 1, as said below
Outputs:
- swapped: float32 [20, 3, 64, 4096], P('rep', None, 'tm', 'space')
- energies: float32 [20, 64], P('rep', 'tm')
Inputs may be any that keep to these rules, and one draw needn't show every extreme that they name: partner[r] is r - 1, r or r + 1, and partner[partner[r]] = r; partner[r] = r + 1 wherever r % 5 = 4 and r + 1 < 20. accept[r] = accept[partner[r]], accept[r] = 0 where partner[r] = r, and accept[r] = 1 wherever r % 5 = 4 and r + 1 < 20.
All inputs are finite; a program needn't handle non-finite values.
Results may differ from a plain program's by a relative error of at most 0.0001.
Values sent between devices are 32-bit elements; how exact they have to be, the bound alone decides.
A program may use at most 64 MiB of HBM per device.

v0:
```python
import jax
import jax.numpy as jnp
from jax import lax
from jax.sharding import PartitionSpec as P

LY = 64


def shifted(x, axis, by):
    size = lax.axis_size(axis)
    return lax.ppermute(x, axis, [(i, (i + by) % size) for i in range(size)])


def extended_2(cells, sides, width):
    for axis, dim in sides:
        count = lax.axis_size(axis)
        head = lax.slice_in_dim(cells, 0, width, axis=dim)
        tail = lax.slice_in_dim(cells, cells.shape[dim] - width, cells.shape[dim], axis=dim)
        cells = jnp.concatenate(
            [
                lax.ppermute(tail, axis, [(i, (i + 1) % count) for i in range(count)]),
                cells,
                lax.ppermute(head, axis, [((i + 1) % count, i) for i in range(count)]),
            ],
            axis=dim,
        )
    return cells


def from_behind(x, axis, by):
    size = lax.axis_size(axis)
    pairs = [(i, i + by) for i in range(size) if 0 <= i + by < size]
    return lax.ppermute(x, axis, pairs)


def choose(extended, offset):
    return jnp.where(
        offset == -1, extended[:-2], jnp.where(offset == 1, extended[2:], extended[1:-1])
    )


def on_device(spins, bond_right, bond_down, betas, time_coupling, thresholds, partner, accept):
    reps, comps, slices, local = spins.shape
    row_len = LY
    first_row = lax.axis_index("space") * (local // row_len)
    first_slice = lax.axis_index("tm") * slices
    first_rep = lax.axis_index("rep") * reps
    lattice_total = local * lax.axis_size("space")
    flat = jnp.arange(local, dtype=jnp.int32)
    column = flat % row_len
    row = flat // row_len + first_row
    level = jnp.arange(slices, dtype=jnp.int32) + first_slice
    parity = (row[None, :] + column[None, :] + level[:, None]) % 2
    above_bonds = shifted(bond_down[local - row_len :], "space", 1)
    bond_up = jnp.concatenate([above_bonds, bond_down[: local - row_len]], axis=0)
    bond_left = jnp.where(
        column == 0, jnp.roll(bond_right, -(row_len - 1)), jnp.roll(bond_right, 1)
    )
    beta_col = betas[:, None, None, None]
    coupling_col = time_coupling[:, None, None, None]
    state = spins
    field_space = jnp.zeros_like(spins)
    for half in range(2):
        planes = extended_2(state, (("tm", 2),), 1)
        lattice_rows = extended_2(state, (("space", 3),), row_len)
        down = lattice_rows[..., 2 * row_len :]
        upper = lattice_rows[..., :local]
        right = jnp.where(
            column == row_len - 1, jnp.roll(state, row_len - 1, axis=3), jnp.roll(state, -1, axis=3)
        )
        left = jnp.where(
            column == 0, jnp.roll(state, -(row_len - 1), axis=3), jnp.roll(state, 1, axis=3)
        )
        field_space = bond_down * down + bond_up * upper + bond_right * right + bond_left * left
        field = beta_col * field_space + coupling_col * (planes[:, :, 2:] + planes[:, :, :-2])
        weight = (thresholds[half].astype(jnp.float32) + 0.5) / 8192.0
        moved = state + weight[:, None] * field
        fresh = moved / jnp.sqrt(0.25 + jnp.sum(moved * moved, axis=1, keepdims=True))
        state = jnp.where(parity == half, fresh, state)
    site_terms = jnp.where(parity == 1, jnp.sum(state * field_space, axis=1), 0.0)
    partial_energy = -jnp.sum(site_terms, axis=-1) / lattice_total
    offset = jnp.where(accept == 1, partner - (first_rep + jnp.arange(reps, dtype=jnp.int32)), 0)
    energy = lax.psum(partial_energy, "space")
    lower_state, lower_energy = from_behind((state[-1:], energy[-1:]), "rep", 1)
    upper_state, upper_energy = from_behind((state[:1], energy[:1]), "rep", -1)
    state_ext = jnp.concatenate([lower_state, state, upper_state], axis=0)
    energy_ext = jnp.concatenate([lower_energy, energy, upper_energy], axis=0)
    swapped = choose(state_ext, offset[:, None, None, None])
    energies = choose(energy_ext, offset[:, None])
    return (swapped, energies)


def solution(mesh):
    placed = (
        P("rep", None, "tm", "space"),
        P("space"),
        P("space"),
        P("rep"),
        P("rep"),
        P(None, "rep", "tm", "space"),
        P("rep"),
        P("rep"),
    )
    return jax.shard_map(
        on_device,
        mesh=mesh,
        in_specs=placed,
        out_specs=(P("rep", None, "tm", "space"), P("rep", "tm")),
        check_vma=False,
    )
```

profile of v0, /device:TPU:0, one launch (start us, length us, event | category | flops | bytes accessed | tf_op | source)
XLA Modules:
  0.0 103.5 jit_solution(7721700712412367964)
XLA Ops:
  0.6 2.7 %copy.73 = f32[5,3,16,2048]{3,0,2,1:T(8,128)S(1)} copy(f32[5,3,16,2048]{3,2,1,0:T(8,128)} %param.8) | data formatting | bytes 3932160 | tf_op args[0]
  3.3 0.8 fusion.52
  4.1 3.0 %collective-permute-start = (f32[5,3,16,64]{3,0,2,1:T(8,128)}, f32[5,3,16,64]{3,0,2,1:T(8,128)}, u32[]{:S(2)}, u32[]{:S(2)}) collective-permute-start(f32[5,3,16,64]{3,0,2,1:T(8,128)} %get-tuple-element.30), channel_id=1, source_target_pairs={{1,0},{0,1},{3,2},{2,3},{5,4},{4,5},{7,6},{6,7},{9,8},{8,9},{11,10... | collective-permute-start | bytes 184328 | tf_op jit(solution)/shard_map/ppermute | solution.py:23
  7.1 0.0 collective-permute-start.2
  7.2 0.8 fusion.57
  7.9 0.9 collective-permute-start.3
  8.8 1.3 %slice.171 = f32[64]{0:T(128)} slice(f32[2048]{0:T(1024)} %param.10), slice={[1984:2048]} | slice | bytes 512 | tf_op jit(solution)/shard_map/slice | solution.py:54
  10.1 1.7 %collective-permute-start.1 = (f32[64]{0:T(128)}, f32[64]{0:T(128)}, u32[]{:S(2)}, u32[]{:S(2)}) collective-permute-start(f32[64]{0:T(128)} %slice.171), channel_id=1, source_target_pairs={{0,1},{1,0},{2,3},{3,2},{4,5},{5,4},{6,7},{7,6},{8,9},{9,8},{10,11... | collective-permute-start | bytes 776 | tf_op jit(solution)/shard_map/ppermute | solution.py:11
  11.8 3.8 %fusion.54 = (f32[5,3,16,1985]{3,0,2,1:T(8,128)}, f32[5,3,16,1985]{3,0,2,1:T(8,128)}) fusion(f32[5,3,16,2048]{3,0,2,1:T(8,128)S(1)} %copy.73), kind=kLoop, calls=%fused_computation.94 | loop fusion | bytes 7622400 | tf_op jit(solution)/shard_map/jit(_roll_static)/slice | solution.py:69
  15.6 3.8 %fusion.55 = (f32[5,3,16,2047]{3,0,2,1:T(8,128)}, f32[5,3,16,2047]{3,0,2,1:T(8,128)}) fusion(f32[5,3,16,2048]{3,0,2,1:T(8,128)S(1)} %copy.73), kind=kLoop, calls=%fused_computation.95 | loop fusion | bytes 7860480 | tf_op jit(solution)/shard_map/jit(_roll_static)/slice | solution.py:69
  19.4 0.1 fusion.53
  19.5 0.8 fusion.56
  20.3 0.7 slice.179
  21.0 0.6 slice.180
  21.6 0.6 slice.181
  22.2 0.6 fusion.38
  22.8 2.5 %multiply_bitcast_fusion = (f32[5,16,2048]{2,1,0:T(8,128)}, f32[5,16,2048]{2,1,0:T(8,128)}) fusion(s32[2,5,16,2048]{3,2,1,0:T(8,128)} %param.13), kind=kLoop, calls=%fused_computation.49 | loop fusion | flops 983040 | bytes 2621440 | tf_op jit(solution)/shard_map/div | solution.py:76
  25.3 0.5 iota_add_fusion
  25.8 0.0 copy-start.11
  25.8 0.0 copy-start.12
  25.8 1.4 %broadcast_compare_fusion = (pred[5]{0:T(512)(128)(4,1)}, s32[5]{0:T(128)S(1)}) fusion(s32[5]{0:T(128)} %param.14, s32[]{:T(128)S(6)} %mul.56, s32[5]{0:T(128)} %param.15), kind=kLoop, calls=%fused_computation.83 | loop fusion | flops 25 | bytes 69 | tf_op jit(solution)/shard_map/eq | solution.py:38
  27.2 0.6 broadcast_compare_fusion.1
  27.8 1.4 %fusion.29 = (pred[16,2048]{1,0:T(8,128)(4,1)}, pred[16,2048]{1,0:T(8,128)(4,1)S(1)}) fusion(s32[16]{0:T(128)} %iota_add_fusion, s32[2048]{0:T(1024)S(1)} %fusion.37), kind=kLoop, calls=%fused_computation.58 | loop fusion | flops 458752 | bytes 73792 | tf_op jit(solution)/shard_map/eq | solution.py:79
  29.2 1.4 %maximum_select_fusion.4 = f32[2048]{0:T(1024)S(1)} fusion(f32[63]{0:T(128)} %slice.180, f32[1985]{0:T(1024)} %slice.179, f32[2047]{0:T(1024)S(1)} %bitcast.6, f32[1]{0:T(128)} %slice.181), kind=kLoop, calls=%fused_computation.79 | loop fusion | flops 20480 | bytes 24576 | tf_op jit(solution)/shard_map/jit(_where)/select_n | solution.py:56
  30.6 1.5 %copy.56 = f32[5,16,2048]{2,0,1:T(8,128)S(1)} copy(f32[5,16,2048]{2,1,0:T(8,128)} %get-tuple-element.43) | data formatting | bytes 1310720 | tf_op jit(solution)/shard_map/div | solution.py:76
  32.1 2.5 %copy.75 = f32[5,16,2048]{2,0,1:T(8,128)} copy(f32[5,16,2048]{2,1,0:T(8,128)} %get-tuple-element.42) | data formatting | bytes 1310720 | tf_op jit(solution)/shard_map/div | solution.py:76
  34.5 0.8 pad_maximum_fusion.12
  35.4 7.4 %multiply_reduce_fusion.2 = (f32[5,16,2048]{2,0,1:T(8,128)S(1)}, f32[5,3,16,2048]{3,0,2,1:T(8,128)S(1)}) fusion(f32[5,3,16,2048]{3,0,2,1:T(8,128)S(1)} %copy.73, f32[5,3,1,2048]{3,0,2,1:T(8,128)} %collective-permute-done.4, f32[5,3,1,2048]{3,0,2,1:T(8,128)} %collective-permute-done.3, f32[5]{0:T(128)S(1)} %copy-done.11, ...), kind=kLoop, calls=%fused_computation.45 | loop fusion | flops 12124160 | bytes 13512744 | tf_op jit(solution)/shard_map/reduce_sum | solution.py:78
  42.8 0.0 copy-start.2
  42.8 0.3 add_sqrt_fusion.1
  43.1 1.3 %copy-done.2 = f32[5,3,16,2048]{3,2,1,0:T(8,128)S(1)} copy-done((f32[5,3,16,2048]{3,2,1,0:T(8,128)S(1)}, f32[5,3,16,2048]{3,2,1,0:T(8,128)}, u32[]{:S(2)}) %copy-start.2) | copy-done | bytes 1966104
  44.4 1.5 %divide_select_fusion.1 = f32[5,3,16,2048]{3,0,2,1:T(8,128)S(1)} fusion(f32[5,3,16,2048]{3,0,2,1:T(8,128)S(1)} %get-tuple-element.15, f32[5,16,2048]{2,0,1:T(8,128)S(1)} %add_sqrt_fusion.1, pred[16,2048]{1,0:T(8,128)(4,1)S(1)} %get-tuple-element.45, f32[5,3,16,2048]{3,2,1,0:T(8,128)S(1)} %copy-done.2), kind=kLoop, calls=%fused_computation.44 | loop fusion | flops 983040 | bytes 6586368 | tf_op jit(solution)/shard_map/jit(_where)/select_n | solution.py:79
  45.9 1.2 %fusion.48 = (f32[5,3,16,1985]{3,0,2,1:T(8,128)S(1)}, f32[5,3,16,1985]{3,0,2,1:T(8,128)S(1)}) fusion(f32[5,3,16,2048]{3,0,2,1:T(8,128)S(1)} %divide_select_fusion.1), kind=kLoop, calls=%fused_computation.88 | loop fusion | bytes 7622400 | tf_op jit(solution)/shard_map/jit(_roll_static)/slice | solution.py:69
  47.1 1.2 %fusion.49 = (f32[5,3,16,2047]{3,0,2,1:T(8,128)S(1)}, f32[5,3,16,2047]{3,0,2,1:T(8,128)S(1)}) fusion(f32[5,3,16,2048]{3,0,2,1:T(8,128)S(1)} %divide_select_fusion.1), kind=kLoop, calls=%fused_computation.89 | loop fusion | bytes 7860480 | tf_op jit(solution)/shard_map/jit(_roll_static)/slice | solution.py:69
  48.4 0.0 copy-start.1
  48.4 0.1 fusion.46
  48.5 0.1 fusion.47
  48.7 0.4 collective-permute-start.5
  49.1 1.7 %collective-permute-start.6 = (f32[5,3,16,64]{3,0,2,1:T(8,128)S(1)}, f32[5,3,16,64]{3,0,2,1:T(8,128)S(1)}, u32[]{:S(2)}, u32[]{:S(2)}) collective-permute-start(f32[5,3,16,64]{3,0,2,1:T(8,128)S(1)} %get-tuple-element.19), channel_id=1, source_target_pairs={{0,1},{1,0},{2,3},{3,2},{4,5},{5,4},{6,7},{7,6},{8,9},{9,8},{10,11... | collective-permute-start | bytes 184328 | tf_op jit(solution)/shard_map/ppermute | solution.py:21
  50.7 0.8 collective-permute-start.7
  51.5 0.1 fusion.50
  51.6 4.9 %collective-permute-done.5 = f32[5,3,16,64]{3,0,2,1:T(8,128)S(1)} collective-permute-done((f32[5,3,16,64]{3,0,2,1:T(8,128)S(1)}, f32[5,3,16,64]{3,0,2,1:T(8,128)S(1)}, u32[]{:S(2)}, u32[]{:S(2)}) %collective-permute-start.5) | collective-permute-done | bytes 61472 | tf_op jit(solution)/shard_map/ppermute | solution.py:23
  56.5 4.1 %collective-permute-done.6 = f32[5,3,16,64]{3,0,2,1:T(8,128)S(1)} collective-permute-done((f32[5,3,16,64]{3,0,2,1:T(8,128)S(1)}, f32[5,3,16,64]{3,0,2,1:T(8,128)S(1)}, u32[]{:S(2)}, u32[]{:S(2)}) %collective-permute-start.6) | collective-permute-done | bytes 61472 | tf_op jit(solution)/shard_map/ppermute | solution.py:21
  60.6 7.1 %multiply_reduce_fusion.1 = (f32[5,16,2048]{2,0,1:T(8,128)S(1)}, f32[5,3,16,2048]{3,0,2,1:T(8,128)}) fusion(f32[5,3,16,2048]{3,0,2,1:T(8,128)S(1)} %divide_select_fusion.1, f32[5,3,1,2048]{3,0,2,1:T(8,128)S(1)} %collective-permute-done.8, f32[5,3,1,2048]{3,0,2,1:T(8,128)S(1)} %collective-permute-done.7, f32[5]{0:T(128)} %param.12, f32[5]{0:T(128)} %param.11, ...), kind=kLoop, calls=%fused_computation.43 | loop fusion | flops 12124160 | bytes 13512744 | tf_op jit(solution)/shard_map/reduce_sum | solution.py:78
  67.7 0.3 add_sqrt_fusion
  68.0 3.7 %multiply_reduce_fusion = (f32[5,16,2048]{2,0,1:T(8,128)S(1)}, f32[5,3,16,2048]{3,0,2,1:T(8,128)S(1)}) fusion(f32[5,3,16,2048]{3,0,2,1:T(8,128)} %get-tuple-element.13, f32[5,3,16,2048]{3,0,2,1:T(8,128)S(1)} %divide_select_fusion.1, f32[5,16,2048]{2,0,1:T(8,128)S(1)} %add_sqrt_fusion, f32[5,3,1,2048]{3,0,2,1:T(8,128)S(1)} %collective-permute-done.8, ...), kind=kLoop, calls=%fused_computation.41 | loop fusion | flops 5734400 | bytes 8142888 | tf_op jit(solution)/shard_map/reduce_sum | solution.py:80
  71.7 0.3 select_reduce_fusion
  72.0 5.0 %psum.7 = f32[5,16]{0,1:T(8,128)S(1)} all-reduce(f32[5,16]{0,1:T(8,128)S(1)} %negate_multiply_fusion), channel_id=1, replica_groups=mesh['rep'=4,'tm'=4,'space'=2] {'space'}, use_global_device_ids=true, to_apply=%region_4.5 | all-reduce | flops 80 | bytes 640 | tf_op jit(solution)/shard_map/psum | solution.py:83
  77.0 0.6 fusion.45
  77.6 0.1 copy.76
  77.7 4.2 %collective-permute-start.9 = (f32[1,3,16,2048]{3,2,1,0:T(8,128)S(1)}, f32[1,3,16,2048]{3,2,1,0:T(8,128)}, u32[]{:S(2)}, u32[]{:S(2)}) collective-permute-start(f32[1,3,16,2048]{3,2,1,0:T(8,128)S(1)} %copy.76), channel_id=1, source_target_pairs={{0,8},{8,16},{16,24},{1,9},{9,17},{17,25},{2,10},{10,18},{18,26},{... | collective-permute-start | bytes 1179656 | tf_op jit(solution)/shard_map/ppermute | solution.py:33
  82.0 0.9 copy.78
  82.8 1.3 %collective-permute-start.10 = (f32[1,3,16,2048]{3,2,1,0:T(8,128)}, f32[1,3,16,2048]{3,2,1,0:T(8,128)}, u32[]{:S(2)}, u32[]{:S(2)}) collective-permute-start(f32[1,3,16,2048]{3,2,1,0:T(8,128)} %copy.78), channel_id=1, source_target_pairs={{8,0},{16,8},{24,16},{9,1},{17,9},{25,17},{10,2},{18,10},{26,18},{... | collective-permute-start | bytes 1179656 | tf_op jit(solution)/shard_map/ppermute | solution.py:33
  84.1 0.1 fusion.58
  84.2 4.5 %collective-permute-start.11 = (f32[1,16]{0,1:T(8,128)S(1)}, f32[1,16]{0,1:T(8,128)S(1)}, u32[]{:S(2)}, u32[]{:S(2)}) collective-permute-start(f32[1,16]{0,1:T(8,128)S(1)} %get-tuple-element.46), channel_id=1, source_target_pairs={{0,8},{8,16},{16,24},{1,9},{9,17},{17,25},{2,10},{10,18},{18,26},{... | collective-permute-start | bytes 200 | tf_op jit(solution)/shard_map/ppermute | solution.py:33
  88.7 1.3 %collective-permute-start.12 = (f32[1,16]{0,1:T(8,128)S(1)}, f32[1,16]{0,1:T(8,128)S(1)}, u32[]{:S(2)}, u32[]{:S(2)}) collective-permute-start(f32[1,16]{0,1:T(8,128)S(1)} %get-tuple-element.47), channel_id=1, source_target_pairs={{8,0},{16,8},{24,16},{9,1},{17,9},{25,17},{10,2},{18,10},{26,18},{... | collective-permute-start | bytes 200 | tf_op jit(solution)/shard_map/ppermute | solution.py:33
  90.0 0.0 collective-permute-done.11
  90.1 4.6 %collective-permute-done.12 = f32[1,16]{0,1:T(8,128)S(1)} collective-permute-done((f32[1,16]{0,1:T(8,128)S(1)}, f32[1,16]{0,1:T(8,128)S(1)}, u32[]{:S(2)}, u32[]{:S(2)}) %collective-permute-start.12) | collective-permute-done | bytes 96 | tf_op jit(solution)/shard_map/ppermute | solution.py:33
  94.7 0.8 fusion.42
  95.4 0.7 copy.81
  96.1 1.4 %copy.77 = f32[1,3,16,2048]{3,0,2,1:T(1,128)S(1)} copy(f32[1,3,16,2048]{3,2,1,0:T(8,128)} %collective-permute-done.9) | data formatting | bytes 786432 | tf_op jit(solution)/shard_map/ppermute | solution.py:33
  97.5 1.4 %copy.79 = f32[1,3,16,2048]{3,0,2,1:T(1,128)S(1)} copy(f32[1,3,16,2048]{3,2,1,0:T(8,128)} %collective-permute-done.10) | data formatting | bytes 786432 | tf_op jit(solution)/shard_map/ppermute | solution.py:33
  98.9 2.2 %fusion.1 = f32[5,3,16,2048]{3,0,2,1:T(8,128)S(1)} fusion(f32[5,3,16,2048]{3,0,2,1:T(8,128)S(1)} %get-tuple-element.9, f32[1,3,16,2048]{3,0,2,1:T(1,128)S(1)} %copy.79, f32[1,3,16,2048]{3,0,2,1:T(1,128)S(1)} %copy.77, pred[5]{0:T(512)(128)(4,1)} %broadcast_compare_fusion.1, pred[5]{0:T(512)(128)(4,1)} %get-tuple-element.10), kind=kLoop, calls=%fused_computation.2 | loop fusion | flops 1966080 | bytes 4718602 | tf_op jit(solution)/shard_map/jit(_where)/select_n | solution.py:37
  101.1 2.4 %copy.80 = f32[5,3,16,2048]{3,2,1,0:T(8,128)} copy(f32[5,3,16,2048]{3,0,2,1:T(8,128)S(1)} %fusion.1) | data formatting | bytes 3932160
  (36 shorter events, 0.1 us)
Async XLA Ops:
  4.1 31.2 %collective-permute-start = (f32[5,3,16,64]{3,0,2,1:T(8,128)}, f32[5,3,16,64]{3,0,2,1:T(8,128)}, u32[]{:S(2)}, u32[]{:S(2)}) collective-permute-start(f32[5,3,16,64]{3,0,2,1:T(8,128)} %get-tuple-element.30), channel_id=1, source_target_pairs={{1,0},{0,1},{3,2},{2,3},{5,4},{4,5},{7,6},{6,7},{9,8},{8,9},{11,10... | collective-permute-start | bytes 184328 | tf_op jit(solution)/shard_map/ppermute | solution.py:23
  7.1 28.2 %collective-permute-start.2 = (f32[5,3,16,64]{3,0,2,1:T(8,128)}, f32[5,3,16,64]{3,0,2,1:T(8,128)}, u32[]{:S(2)}, u32[]{:S(2)}) collective-permute-start(f32[5,3,16,64]{3,0,2,1:T(8,128)} %get-tuple-element.31), channel_id=1, source_target_pairs={{0,1},{1,0},{2,3},{3,2},{4,5},{5,4},{6,7},{7,6},{8,9},{9,8},{10,11... | collective-permute-start | bytes 184328 | tf_op jit(solution)/shard_map/ppermute | solution.py:21
  7.9 27.4 %collective-permute-start.3 = (f32[5,3,1,2048]{3,0,2,1:T(8,128)}, f32[5,3,1,2048]{3,0,2,1:T(8,128)}, u32[]{:S(2)}, u32[]{:S(2)}) collective-permute-start(f32[5,3,1,2048]{3,0,2,1:T(8,128)} %get-tuple-element.40), channel_id=1, source_target_pairs={{2,0},{4,2},{6,4},{0,6},{3,1},{5,3},{7,5},{1,7},{10,8},{12,10},{14... | collective-permute-start | bytes 368648 | tf_op jit(solution)/shard_map/ppermute | solution.py:23
  8.8 26.6 %collective-permute-start.4 = (f32[5,3,1,2048]{3,0,2,1:T(8,128)}, f32[5,3,1,2048]{3,0,2,1:T(8,128)}, u32[]{:S(2)}, u32[]{:S(2)}) collective-permute-start(f32[5,3,1,2048]{3,0,2,1:T(8,128)} %get-tuple-element.41), channel_id=1, source_target_pairs={{0,2},{2,4},{4,6},{6,0},{1,3},{3,5},{5,7},{7,1},{8,10},{10,12},{12... | collective-permute-start | bytes 368648 | tf_op jit(solution)/shard_map/ppermute | solution.py:21
  10.1 24.4 %collective-permute-start.1 = (f32[64]{0:T(128)}, f32[64]{0:T(128)}, u32[]{:S(2)}, u32[]{:S(2)}) collective-permute-start(f32[64]{0:T(128)} %slice.171), channel_id=1, source_target_pairs={{0,1},{1,0},{2,3},{3,2},{4,5},{5,4},{6,7},{7,6},{8,9},{9,8},{10,11... | collective-permute-start | bytes 776 | tf_op jit(solution)/shard_map/ppermute | solution.py:11
  15.6 4.7 %copy-start.6 = (f32[2048]{0:T(1024)S(1)}, f32[2048]{0:T(1024)}, u32[]{:S(2)}) copy-start(f32[2048]{0:T(1024)} %param.9) | copy-start | bytes 24580
  25.8 9.6 %copy-start = (f32[5,3,16,1985]{3,0,2,1:T(8,128)S(1)}, f32[5,3,16,1985]{3,0,2,1:T(8,128)}, u32[]{:S(2)}) copy-start(f32[5,3,16,1985]{3,0,2,1:T(8,128)} %get-tuple-element.34) | copy-start | bytes 5716804
  25.8 9.6 %copy-start.3 = (f32[5,3,16,1]{3,0,2,1:T(8,128)S(1)}, f32[5,3,16,1]{3,0,2,1:T(8,128)}, u32[]{:S(2)}) copy-start(f32[5,3,16,1]{3,0,2,1:T(8,128)} %get-tuple-element.38) | copy-start | bytes 2884
  25.8 9.6 %copy-start.4 = (f32[5,3,16,1]{3,0,2,1:T(8,128)S(1)}, f32[5,3,16,1]{3,0,2,1:T(8,128)}, u32[]{:S(2)}) copy-start(f32[5,3,16,1]{3,0,2,1:T(8,128)} %get-tuple-element.39) | copy-start | bytes 2884
  25.8 9.6 %copy-start.9 = (pred[2048]{0:T(1024)(128)(4,1)S(1)}, pred[2048]{0:T(1024)(128)(4,1)}, u32[]{:S(2)}) copy-start(pred[2048]{0:T(1024)(128)(4,1)} %fusion.38) | copy-start | bytes 6148
  25.8 9.6 %copy-start.11 = (f32[5]{0:T(128)S(1)}, f32[5]{0:T(128)}, u32[]{:S(2)}) copy-start(f32[5]{0:T(128)} %param.12) | copy-start | bytes 64
  25.8 9.6 %copy-start.12 = (f32[5]{0:T(128)S(1)}, f32[5]{0:T(128)}, u32[]{:S(2)}) copy-start(f32[5]{0:T(128)} %param.11) | copy-start | bytes 64
  30.6 12.2 %copy-start.10 = (pred[2048]{0:T(1024)(128)(4,1)}, pred[2048]{0:T(1024)(128)(4,1)S(1)}, u32[]{:S(2)}) copy-start(pred[2048]{0:T(1024)(128)(4,1)S(1)} %fusion.39) | copy-start | bytes 6148
  35.3 7.5 %copy-start.8 = (f32[2048]{0:T(1024)}, f32[2048]{0:T(1024)S(1)}, u32[]{:S(2)}) copy-start(f32[2048]{0:T(1024)S(1)} %pad_maximum_fusion.12) | copy-start | bytes 24580
  42.8 1.5 %copy-start.2 = (f32[5,3,16,2048]{3,2,1,0:T(8,128)S(1)}, f32[5,3,16,2048]{3,2,1,0:T(8,128)}, u32[]{:S(2)}) copy-start(f32[5,3,16,2048]{3,2,1,0:T(8,128)} %param.8) | copy-start | bytes 5898244
  48.4 12.2 %copy-start.1 = (f32[5,16,2048]{2,0,1:T(8,128)S(1)}, f32[5,16,2048]{2,0,1:T(8,128)}, u32[]{:S(2)}) copy-start(f32[5,16,2048]{2,0,1:T(8,128)} %copy.75) | copy-start | bytes 1966084
  48.4 12.2 %copy-start.7 = (f32[2048]{0:T(1024)S(1)}, f32[2048]{0:T(1024)}, u32[]{:S(2)}) copy-start(f32[2048]{0:T(1024)} %param.10) | copy-start | bytes 24580
  48.7 7.8 %collective-permute-start.5 = (f32[5,3,16,64]{3,0,2,1:T(8,128)S(1)}, f32[5,3,16,64]{3,0,2,1:T(8,128)S(1)}, u32[]{:S(2)}, u32[]{:S(2)}) collective-permute-start(f32[5,3,16,64]{3,0,2,1:T(8,128)S(1)} %get-tuple-element.18), channel_id=1, source_target_pairs={{1,0},{0,1},{3,2},{2,3},{5,4},{4,5},{7,6},{6,7},{9,8},{8,9},{11,10... | collective-permute-start | bytes 184328 | tf_op jit(solution)/shard_map/ppermute | solution.py:23
  49.1 11.5 %collective-permute-start.6 = (f32[5,3,16,64]{3,0,2,1:T(8,128)S(1)}, f32[5,3,16,64]{3,0,2,1:T(8,128)S(1)}, u32[]{:S(2)}, u32[]{:S(2)}) collective-permute-start(f32[5,3,16,64]{3,0,2,1:T(8,128)S(1)} %get-tuple-element.19), channel_id=1, source_target_pairs={{0,1},{1,0},{2,3},{3,2},{4,5},{5,4},{6,7},{7,6},{8,9},{9,8},{10,11... | collective-permute-start | bytes 184328 | tf_op jit(solution)/shard_map/ppermute | solution.py:21
  50.7 9.8 %collective-permute-start.7 = (f32[5,3,1,2048]{3,0,2,1:T(8,128)S(1)}, f32[5,3,1,2048]{3,0,2,1:T(8,128)S(1)}, u32[]{:S(2)}, u32[]{:S(2)}) collective-permute-start(f32[5,3,1,2048]{3,0,2,1:T(8,128)S(1)} %get-tuple-element.28), channel_id=1, source_target_pairs={{2,0},{4,2},{6,4},{0,6},{3,1},{5,3},{7,5},{1,7},{10,8},{12,10},{14... | collective-permute-start | bytes 368648 | tf_op jit(solution)/shard_map/ppermute | solution.py:23
  51.5 9.1 %collective-permute-start.8 = (f32[5,3,1,2048]{3,0,2,1:T(8,128)S(1)}, f32[5,3,1,2048]{3,0,2,1:T(8,128)S(1)}, u32[]{:S(2)}, u32[]{:S(2)}) collective-permute-start(f32[5,3,1,2048]{3,0,2,1:T(8,128)S(1)} %get-tuple-element.29), channel_id=1, source_target_pairs={{0,2},{2,4},{4,6},{6,0},{1,3},{3,5},{5,7},{7,1},{8,10},{10,12},{12... | collective-permute-start | bytes 368648 | tf_op jit(solution)/shard_map/ppermute | solution.py:21
  68.0 3.7 %copy-start.5 = (pred[16,2048]{1,0:T(8,128)(4,1)S(1)}, pred[16,2048]{1,0:T(8,128)(4,1)}, u32[]{:S(2)}) copy-start(pred[16,2048]{1,0:T(8,128)(4,1)} %get-tuple-element.44) | copy-start | bytes 98308
  77.7 18.4 %collective-permute-start.9 = (f32[1,3,16,2048]{3,2,1,0:T(8,128)S(1)}, f32[1,3,16,2048]{3,2,1,0:T(8,128)}, u32[]{:S(2)}, u32[]{:S(2)}) collective-permute-start(f32[1,3,16,2048]{3,2,1,0:T(8,128)S(1)} %copy.76), channel_id=1, source_target_pairs={{0,8},{8,16},{16,24},{1,9},{9,17},{17,25},{2,10},{10,18},{18,26},{... | collective-permute-start | bytes 1179656 | tf_op jit(solution)/shard_map/ppermute | solution.py:33
  82.8 14.7 %collective-permute-start.10 = (f32[1,3,16,2048]{3,2,1,0:T(8,128)}, f32[1,3,16,2048]{3,2,1,0:T(8,128)}, u32[]{:S(2)}, u32[]{:S(2)}) collective-permute-start(f32[1,3,16,2048]{3,2,1,0:T(8,128)} %copy.78), channel_id=1, source_target_pairs={{8,0},{16,8},{24,16},{9,1},{17,9},{25,17},{10,2},{18,10},{26,18},{... | collective-permute-start | bytes 1179656 | tf_op jit(solution)/shard_map/ppermute | solution.py:33
  84.2 5.9 %collective-permute-start.11 = (f32[1,16]{0,1:T(8,128)S(1)}, f32[1,16]{0,1:T(8,128)S(1)}, u32[]{:S(2)}, u32[]{:S(2)}) collective-permute-start(f32[1,16]{0,1:T(8,128)S(1)} %get-tuple-element.46), channel_id=1, source_target_pairs={{0,8},{8,16},{16,24},{1,9},{9,17},{17,25},{2,10},{10,18},{18,26},{... | collective-permute-start | bytes 200 | tf_op jit(solution)/shard_map/ppermute | solution.py:33
  88.7 5.9 %collective-permute-start.12 = (f32[1,16]{0,1:T(8,128)S(1)}, f32[1,16]{0,1:T(8,128)S(1)}, u32[]{:S(2)}, u32[]{:S(2)}) collective-permute-start(f32[1,16]{0,1:T(8,128)S(1)} %get-tuple-element.47), channel_id=1, source_target_pairs={{8,0},{16,8},{24,16},{9,1},{17,9},{25,17},{10,2},{18,10},{26,18},{... | collective-permute-start | bytes 200 | tf_op jit(solution)/shard_map/ppermute | solution.py:33
where the time goes:
time: 104 us
  other arithmetic  32.6 us (31%)
  local copies, waits for them, and re-layouts  31.7 us (30%)
  starting transfers between devices  19.8 us (19%)
  waiting for transfers between devices  13.6 us (13%)
  blocking collectives  4.96 us (5%)
    reduce_sum x2, other arithmetic, on_device(): jnp.sum(moved * moved, axis=1, keepdims=True)  14.5 us
    ppermute x4, starting transfers between devices, from_behind(): return lax.ppermute(x, axis, pairs)  11.4 us
    unnamed x29, local copies, waits for them, and re-layouts  7.1 us
    slice x4, local copies, waits for them, and re-layouts, on_device(): jnp.roll(state, -1, axis=3)  5.96 us
    slice x4, local copies, waits for them, and re-layouts, on_device(): jnp.roll(state, row_len - 1, axis=3)  5.28 us
    ppermute x4, starting transfers between devices, extended_2(): lax.ppermute(head, axis, [((i + 1) % count, i) for i in range(count)])  5.05 us
    psum x1, blocking collectives, on_device(): energy = lax.psum(partial_energy, 'space')  4.96 us
    ppermute x4, waiting for transfers between devices, extended_2(): lax.ppermute(head, axis, [((i + 1) % count, i) for i in range(count)])  4.87 us
  transfers between devices with their start and end apart: 13, of which 3 were waited for; matrix products, arithmetic and copies ran while one was open for 28% of the time, Pallas kernels for 0%

commit v1 on v0

v1 whole, which is shorter than its diff:
```python
import functools

import jax
import jax.numpy as jnp
from jax import lax
from jax.experimental import pallas as pl
from jax.experimental.pallas import tpu as pltpu
from jax.sharding import PartitionSpec as P

LY = 64
W = 2 * LY
MESH = pl.DeviceIdType.MESH


def kernel(
    sizes,
    betas, tcs, partner, accept, bond_right, bond_down, spins, thr,
    out, out_e,
    S, F, TH, OUT, HS, HT, ET, BO, BDS, BDH, CE, RC, EA, ER, EN,
    load_sem, halo_send, halo_recv, bond_sem, rep_send, rep_recv,
    en_send, en_recv, er_send, er_recv, out_sem,
):
    nrep, ntm, nsp = sizes
    R, C, T, L = S.shape
    NJ = L // W
    total = L * nsp
    ri, ti, si = lax.axis_index("rep"), lax.axis_index("tm"), lax.axis_index("space")
    has_low = ri > 0
    has_up = ri < nrep - 1
    t_prev, t_next = lax.rem(ti + ntm - 1, ntm), lax.rem(ti + 1, ntm)
    s_prev, s_next = lax.rem(si + nsp - 1, nsp), lax.rem(si + 1, nsp)
    r_up, r_low = lax.rem(ri + 1, nrep), lax.rem(ri + nrep - 1, nrep)

    def order(i):
        return lax.rem(i + R - 1, R)

    def loads(r):
        return (
            pltpu.make_async_copy(spins.at[r], S.at[r], load_sem.at[0, r]),
            pltpu.make_async_copy(thr.at[:, r], TH.at[:, r], load_sem.at[1, r]),
        )

    for i in range(R):
        a, b = loads((i + R - 1) % R)
        a.start()
        b.start()

    barrier = pltpu.get_barrier_semaphore()

    def greet(dev):
        pl.semaphore_signal(barrier, inc=1, device_id=dev, device_id_type=MESH)

    greet((ri, t_prev, si))
    greet((ri, t_next, si))
    for k in range(1, nsp):
        greet((ri, ti, lax.rem(si + k, nsp)))

    @pl.when(has_low)
    def _():
        for k in range(nsp):
            greet((r_low, ti, lax.rem(si + k, nsp)))

    @pl.when(has_up)
    def _():
        for k in range(nsp):
            greet((r_up, ti, lax.rem(si + k, nsp)))

    def halo(p, k, r):
        if k == 0:
            src, dst, dev = ET.at[p, 0, r], HT.at[p, 1, r], (ri, t_prev, si)
        elif k == 1:
            src, dst, dev = ET.at[p, 1, r], HT.at[p, 0, r], (ri, t_next, si)
        else:
            base = spins if p == 0 else S
            lo = 0 if k == 2 else L - W
            src = base.at[r, :, :, pl.ds(lo, W)]
            if k == 2:
                dst, dev = HS.at[p, 1, r], (ri, ti, s_prev)
            else:
                dst, dev = HS.at[p, 0, r], (ri, ti, s_next)
        return pltpu.make_async_remote_copy(
            src, dst, halo_send.at[p, k, r], halo_recv.at[p, k, r],
            device_id=dev, device_id_type=MESH,
        )

    def rep_copy(p, up):
        u = 1 if up else 0
        return pltpu.make_async_remote_copy(
            CE.at[u, p], RC.at[u, p], rep_send.at[u, p], rep_recv.at[u, p],
            device_id=(r_up if up else r_low, ti, si), device_id_type=MESH,
        )

    def en_copy(k, r):
        return pltpu.make_async_remote_copy(
            EA.at[0, r], EA.at[k, r], en_send.at[k, r], en_recv.at[k, r],
            device_id=(ri, ti, lax.rem(si + k, nsp)), device_id_type=MESH,
        )

    def er_copy(k, up):
        u = 1 if up else 0
        return pltpu.make_async_remote_copy(
            EA.at[0, R - 1 if up else 0], ER.at[u, k], er_send.at[u, k], er_recv.at[u, k],
            device_id=(r_up if up else r_low, ti, lax.rem(si + k, nsp)), device_id_type=MESH,
        )

    bond_copy = pltpu.make_async_remote_copy(
        BDS, BDH, bond_sem.at[0], bond_sem.at[1], device_id=(ri, ti, s_next), device_id_type=MESH
    )

    lane = lax.broadcasted_iota(jnp.int32, (8, W), 1)
    sub8 = lax.broadcasted_iota(jnp.int32, (8, W), 0)
    lane1 = lax.broadcasted_iota(jnp.int32, (T, W), 1)
    sub = lax.broadcasted_iota(jnp.int32, (T, W), 0)
    first_row = si * (L // LY)
    first_slice = ti * T
    lo8 = lane < LY
    lo_half = lane1 < LY
    col0 = lane1 % LY == 0
    col_last = lane1 % LY == LY - 1
    t_first = sub == 0
    t_last = sub == T - 1
    even = (lane1 // LY + lane1 % LY + sub + first_row + first_slice) % 2 == 0
    even8 = (lane // LY + lane % LY + sub8 + first_row + first_slice) % 2 == 0

    def row(ref, j):
        return jnp.broadcast_to(ref[pl.ds(j * W, W)].reshape(1, W), (8, W))

    BDS[...] = row(bond_down, NJ - 1)
    count = 2 + (nsp - 1) + nsp * (has_low.astype(jnp.int32) + has_up.astype(jnp.int32))
    pl.semaphore_wait(barrier, count)

    bond_copy.start()
    for i in range(R):
        for k in (2, 3):
            halo(0, k, (i + R - 1) % R).start()

    def edges(i, carry):
        r = order(i)
        loads(r)[0].wait()
        for c in range(C):
            ET[0, 0, r, c] = S[r, c, 0:1, :]
            ET[0, 1, r, c] = S[r, c, T - 1 : T, :]
        halo(0, 0, r).start()
        halo(0, 1, r).start()
        return carry

    lax.fori_loop(0, R, edges, 0)

    bond_copy.wait()
    prev_rot = pltpu.roll(BDH[...], LY, 1)
    for j in range(NJ):
        bd = row(bond_down, j)
        br = row(bond_right, j)
        rot = pltpu.roll(bd, LY, 1)
        BO[0, :, pl.ds(j * W, W)] = bd
        BO[1, :, pl.ds(j * W, W)] = jnp.where(lo8, prev_rot, rot)
        BO[2, :, pl.ds(j * W, W)] = br
        rot_r = pltpu.roll(br, LY, 1)
        BO[3, :, pl.ds(j * W, W)] = pltpu.roll(jnp.where(lane % LY == LY - 1, rot_r, br), 1, 1)
        prev_rot = rot

    def tall(x):
        return jnp.concatenate([x] * (T // 8), axis=0)

    def sweep(p, r, pack_to):
        beta = betas[r]
        tc = tcs[r]
        rots = {}

        def rot(j):
            if j not in rots:
                if j < 0:
                    rots[j] = [pltpu.roll(HS[p, 0, r, c], LY, 1) for c in range(C)]
                elif j >= NJ:
                    rots[j] = [pltpu.roll(HS[p, 1, r, c], LY, 1) for c in range(C)]
                else:
                    rots[j] = [pltpu.roll(S[r, c, :, pl.ds(j * W, W)], LY, 1) for c in range(C)]
            return rots[j]

        acc = jnp.zeros((T, W), jnp.float32)
        for j in range(NJ):
            at = pl.ds(j * W, W)
            before, here, after = rot(j - 1), rot(j), rot(j + 1)
            bd, bu, br, bl = (tall(BO[q, :, at]) for q in range(4))
            weight = (TH[p, r, :, at].astype(jnp.float32) + 0.5) * (1.0 / 8192.0)
            old, fields, moved = [], [], []
            for c in range(C):
                s = S[r, c, :, at]
                down = jnp.where(lo_half, here[c], after[c])
                up = jnp.where(lo_half, before[c], here[c])
                right = pltpu.roll(jnp.where(col0, here[c], s), W - 1, 1)
                left = pltpu.roll(jnp.where(col_last, here[c], s), 1, 1)
                fs = bd * down + bu * up + br * right + bl * left
                later = jnp.where(t_last, HT[p, 1, r, c, :, at], pltpu.roll(s, T - 1, 0))
                earlier = jnp.where(t_first, HT[p, 0, r, c, :, at], pltpu.roll(s, 1, 0))
                field = beta * fs + tc * (later + earlier)
                old.append(s)
                fields.append(fs)
                moved.append(s + weight * field)
            norm = lax.rsqrt(0.25 + (moved[0] * moved[0] + moved[1] * moved[1] + moved[2] * moved[2]))
            dot = None
            for c in range(C):
                fresh = moved[c] * norm
                if p == 0:
                    new = jnp.where(even, fresh, old[c])
                    S[r, c, :, at] = new
                    ET[1, 0, r, c, :, at] = new[0:1]
                    ET[1, 1, r, c, :, at] = new[T - 1 : T]
                else:
                    new = jnp.where(even, old[c], fresh)
                    F[r, c, :, at] = new
                    term = fresh * fields[c]
                    dot = term if dot is None else dot + term
                if pack_to is not None:
                    for b in range(T // 16):
                        a0 = new[16 * b : 16 * b + 8]
                        a1 = pltpu.roll(new[16 * b + 8 : 16 * b + 16], 1, 0)
                        kept = jnp.where(even8, a0, a1) if p == 0 else jnp.where(even8, a1, a0)
                        CE[pack_to, p, c, pl.ds(8 * b, 8), at] = kept
            if p == 1:
                acc = acc + jnp.where(even, 0.0, dot)
            del rots[j - 1]
        if p == 1:
            EA[0, r] = acc

    def halo_wait(p, r):
        for k in range(4):
            halo(p, k, r).wait_recv()

    def after_first(r):
        for k in range(4):
            halo(1, k, r).start()

    def first(r, pack_to):
        loads(r)[1].wait()
        halo_wait(0, r)
        sweep(0, r, pack_to)
        after_first(r)

    def edge_first(i, carry):
        r = order(i)
        first(r, 1 - i)

        @pl.when((i == 0) & has_up)
        def _():
            rep_copy(0, True).start()

        @pl.when((i == 1) & has_low)
        def _():
            rep_copy(0, False).start()

        return carry

    def inner_first(r, carry):
        first(r, None)
        return carry

    lax.fori_loop(0, 2, edge_first, 0)
    lax.fori_loop(1, R - 1, inner_first, 0)

    def second(r, pack_to):
        halo_wait(1, r)
        sweep(1, r, pack_to)
        for k in range(1, nsp):
            en_copy(k, r).start()

    def edge_second(i, carry):
        r = order(i)
        second(r, 1 - i)

        @pl.when((i == 0) & has_up)
        def _():
            for k in range(nsp):
                er_copy(k, True).start()
            rep_copy(1, True).start()

        @pl.when((i == 1) & has_low)
        def _():
            for k in range(nsp):
                er_copy(k, False).start()
            rep_copy(1, False).start()

        return carry

    def inner_second(r, carry):
        second(r, None)
        return carry

    lax.fori_loop(0, 2, edge_second, 0)
    lax.fori_loop(1, R - 1, inner_second, 0)

    def source(r):
        src = jnp.where(accept[r] == 1, partner[r] - ri * R, r)
        return jnp.clip(src, 0, R - 1)

    def put(r, src):
        for c in range(C):
            OUT[r, c] = F[src, c]

    def write(r):
        return pltpu.make_async_copy(OUT.at[r], out.at[r], out_sem.at[r])

    def inner_put(r, carry):
        put(r, source(r))
        write(r).start()
        return carry

    lax.fori_loop(1, R - 1, inner_put, 0)

    def unpack(u, r):
        for c in range(C):
            for j in range(NJ):
                at = pl.ds(j * W, W)
                for b in range(T // 16):
                    e = RC[u, 0, c, pl.ds(8 * b, 8), at]
                    o = RC[u, 1, c, pl.ds(8 * b, 8), at]
                    OUT[r, c, pl.ds(16 * b, 8), at] = jnp.where(even8, e, o)
                    OUT[r, c, pl.ds(16 * b + 8, 8), at] = pltpu.roll(jnp.where(even8, o, e), 7, 0)

    def lines(a):
        ones = jnp.ones((8, W), jnp.float32)
        sums = lax.dot_general(
            ones, a, (((1,), (1,)), ((), ())),
            precision=lax.Precision.HIGHEST, preferred_element_type=jnp.float32,
        )
        return -sums * (1.0 / total)

    for r in range(R):
        for k in range(1, nsp):
            en_copy(k, r).wait()
        a = EA[0, r]
        for k in range(1, nsp):
            a = a + EA[k, r]
        EN[r] = lines(a)

    for r in range(R):
        out_e[pl.ds(r, 1), :] = EN[source(r)][0:1]

    def edge_sum(u):
        a = ER[u, 0]
        for k in range(1, nsp):
            a = a + ER[u, k]
        return lines(a)[0:1]

    @pl.when(has_low)
    def _():
        for k in range(nsp):
            er_copy(k, True).wait_recv()
        out_e[pl.ds(0, 1), :] = edge_sum(1)
        rep_copy(0, True).wait_recv()
        rep_copy(1, True).wait_recv()
        unpack(1, 0)

    @pl.when(jnp.logical_not(has_low))
    def _():
        put(0, source(0))

    write(0).start()

    @pl.when(has_up)
    def _():
        for k in range(nsp):
            er_copy(k, False).wait_recv()
        out_e[pl.ds(R - 1, 1), :] = edge_sum(0)
        rep_copy(0, False).wait_recv()
        rep_copy(1, False).wait_recv()
        unpack(0, R - 1)

    @pl.when(jnp.logical_not(has_up))
    def _():
        put(R - 1, source(R - 1))

    write(R - 1).start()

    def drain(r, carry):
        for p in range(2):
            for k in range(4):
                halo(p, k, r).wait_send()
        write(r).wait()
        return carry

    lax.fori_loop(0, R, drain, 0)

    def sent(up):
        for k in range(nsp):
            er_copy(k, up).wait_send()
        for p in range(2):
            rep_copy(p, up).wait_send()

    pl.when(has_up)(lambda: sent(True))
    pl.when(has_low)(lambda: sent(False))


def on_device(sizes, spins, bond_right, bond_down, betas, time_coupling, thresholds, partner, accept):
    R, C, T, L = spins.shape
    nsp = sizes[2]
    f32 = jnp.float32
    vm, sm, any_ = (pl.BlockSpec(memory_space=m) for m in (pltpu.VMEM, pltpu.SMEM, pl.ANY))
    dma = pltpu.SemaphoreType.DMA
    return pl.pallas_call(
        functools.partial(kernel, sizes),
        out_shape=(
            jax.ShapeDtypeStruct((R, C, T, L), f32),
            jax.ShapeDtypeStruct((R, T), f32),
        ),
        in_specs=[sm, sm, sm, sm, vm, vm, any_, any_],
        out_specs=(any_, vm),
        scratch_shapes=[
            pltpu.VMEM((R, C, T, L), f32),
            pltpu.VMEM((R, C, T, L), f32),
            pltpu.VMEM((2, R, T, L), jnp.int32),
            pltpu.VMEM((R, C, T, L), f32),
            pltpu.VMEM((2, 2, R, C, T, W), f32),
            pltpu.VMEM((2, 2, R, C, 1, L), f32),
            pltpu.VMEM((2, 2, R, C, 1, L), f32),
            pltpu.VMEM((4, 8, L), f32),
            pltpu.VMEM((8, W), f32),
            pltpu.VMEM((8, W), f32),
            pltpu.VMEM((2, 2, C, T // 2, L), f32),
            pltpu.VMEM((2, 2, C, T // 2, L), f32),
            pltpu.VMEM((nsp, R, T, W), f32),
            pltpu.VMEM((2, nsp, T, W), f32),
            pltpu.VMEM((R, 8, T), f32),
            dma((2, R)),
            dma((2, 4, R)),
            dma((2, 4, R)),
            dma((2,)),
            dma((2, 2)),
            dma((2, 2)),
            dma((nsp, R)),
            dma((nsp, R)),
            dma((2, nsp)),
            dma((2, nsp)),
            dma((R,)),
        ],
        compiler_params=pltpu.CompilerParams(
            collective_id=0, has_side_effects=True, vmem_limit_bytes=56 * 1024 * 1024
        ),
        name="sweep_exchange",
    )(betas, time_coupling, partner, accept, bond_right, bond_down, spins, thresholds)


def solution(mesh):
    placed = (
        P("rep", None, "tm", "space"),
        P("space"),
        P("space"),
        P("rep"),
        P("rep"),
        P(None, "rep", "tm", "space"),
        P("rep"),
        P("rep"),
    )
    sizes = (mesh.shape["rep"], mesh.shape["tm"], mesh.shape["space"])
    return jax.shard_map(
        functools.partial(on_device, sizes),
        mesh=mesh,
        in_specs=placed,
        out_specs=(P("rep", None, "tm", "space"), P("rep", "tm")),
        check_vma=False,
    )
```

time: 104 us -> 28.2 us (0.27)
  other arithmetic: 32.6 us -> 0 us
  local copies, waits for them, and re-layouts: 31.7 us -> 3.62 us
  Pallas kernels: 0 us -> 23.7 us
  starting transfers between devices: 19.8 us -> 0 us
  waiting for transfers between devices: 13.6 us -> 0 us
  blocking collectives: 4.96 us -> 0 us
    pallas_call x0 -> x1, Pallas kernels: none -> 23.7 us  [on_device(): pl.pallas_call(functools.partial(kernel, sizes), out_shape=(jax.ShapeDtyp...]
    ppermute x13 -> x0, starting transfers between devices: 19.8 us -> none  [the longest x4 11.4 us: from_behind(): return lax.ppermute(x, axis, pairs)]
    reduce_sum x4 -> x0, other arithmetic: 18.5 us -> none  [the longest x2 14.5 us: on_device(): jnp.sum(moved * moved, axis=1, keepdims=True)]
    slice x20 -> x0, local copies, waits for them, and re-layouts: 17.8 us -> none  [the longest x4 5.96 us: on_device(): jnp.roll(state, -1, axis=3)]
    ppermute x13 -> x0, waiting for transfers between devices: 13.6 us -> none  [the longest x4 4.87 us: extended_2(): lax.ppermute(head, axis, [((i + 1) % count, i) for i in range(count)])]
    select_n x4 -> x0, other arithmetic: 5.84 us -> none  [the longest x2 2.92 us: choose(): jnp.where(offset == -1, extended[:-2], jnp.where(offset == 1, extended[2:...]
    psum x1 -> x0, blocking collectives: 4.96 us -> none  [on_device(): energy = lax.psum(partial_energy, 'space')]
    div x2 -> x0, local copies, waits for them, and re-layouts: 3.96 us -> none  [on_device(): weight = (thresholds[half].astype(jnp.float32) + 0.5) / 8192.0]
  transfers between devices with their start and end apart: 13 -> 0, of which waited for: 3 -> 0; matrix products, arithmetic and copies ran while one was open for 28% -> 0% of each run, Pallas kernels for 0% -> 0%
where the time goes in v1:
time: 28.2 us; the launch traced here: 28 us
  Pallas kernels  23.7 us (84%)
  local copies, waits for them, and re-layouts  3.62 us (13%)
  between operations  0.65 us (2%)
    pallas_call x1, Pallas kernels, on_device(): pl.pallas_call(functools.partial(kernel, sizes), out_shape=(jax.ShapeDtyp...  23.7 us
    unnamed x4, local copies, waits for them, and re-layouts  3.62 us

profile of v1, /device:TPU:0, one launch (start us, length us, event | category | flops | bytes accessed | tf_op | source)
XLA Modules:
  0.0 28.0 jit_solution(2011621995485105147)
XLA Ops:
  0.6 23.7 %sweep_exchange.1 = (f32[5,3,16,2048]{3,2,1,0:T(8,128)}, f32[5,16]{1,0:T(8,128)}) custom-call(f32[5]{0:T(128)} %betas.1, f32[5]{0:T(128)} %tcs.1, s32[5]{0:T(128)} %partner.1, s32[5]{0:T(128)} %accept.1, f32[2048]{0:T(1024)} %bond_right.1, f32[2048]{0:T(1024)} %bond_down.1, f32[5,3,16,2048]{3,2,1,0:T(8,128)} %spins.1, s32[2,5,16,2048]{3,2,1,0:T(8,128)} %thr.1), custom_call_target="tpu_custom_call" | custom-call | tf_op jit(solution)/shard_map/sweep_exchange/pallas_call | solution.py:400
  24.3 0.0 copy-start
  24.3 3.0 %copy.12 = f32[5,3,16,2048]{3,2,1,0:T(8,128)} copy(f32[5,3,16,2048]{3,2,1,0:T(8,128)} %get-tuple-element.4) | data formatting | bytes 3932160
  27.4 0.0 copy-done
  27.4 0.6 %copy.13 = f32[5,16]{1,0:T(8,128)} copy(f32[5,16]{1,0:T(8,128)S(1)} %copy-done) | data formatting | bytes 640
Async XLA Ops:
  24.3 3.0 %copy-start = (f32[5,16]{1,0:T(8,128)S(1)}, f32[5,16]{1,0:T(8,128)}, u32[]{:S(2)}) copy-start(f32[5,16]{1,0:T(8,128)} %get-tuple-element.5) | copy-start | bytes 964

commit v2 on v1

--- a/solution.py
+++ b/solution.py
@@ -15,10 +15,10 @@
 def kernel(
     sizes,
     betas, tcs, partner, accept, bond_right, bond_down, spins, thr,
-    out, out_e,
-    S, F, TH, OUT, HS, HT, ET, BO, BDS, BDH, CE, RC, EA, ER, EN,
+    OUT, RC, out_e,
+    S, F, TH, HS, HT, ET, BO, BDS, BDH, CE, EA, ER, EN,
     load_sem, halo_send, halo_recv, bond_sem, rep_send, rep_recv,
-    en_send, en_recv, er_send, er_recv, out_sem,
+    en_send, en_recv, er_send, er_recv,
 ):
     nrep, ntm, nsp = sizes
     R, C, T, L = S.shape
@@ -297,25 +297,11 @@
         for c in range(C):
             OUT[r, c] = F[src, c]
 
-    def write(r):
-        return pltpu.make_async_copy(OUT.at[r], out.at[r], out_sem.at[r])
-
     def inner_put(r, carry):
         put(r, source(r))
-        write(r).start()
         return carry
 
     lax.fori_loop(1, R - 1, inner_put, 0)
-
-    def unpack(u, r):
-        for c in range(C):
-            for j in range(NJ):
-                at = pl.ds(j * W, W)
-                for b in range(T // 16):
-                    e = RC[u, 0, c, pl.ds(8 * b, 8), at]
-                    o = RC[u, 1, c, pl.ds(8 * b, 8), at]
-                    OUT[r, c, pl.ds(16 * b, 8), at] = jnp.where(even8, e, o)
-                    OUT[r, c, pl.ds(16 * b + 8, 8), at] = pltpu.roll(jnp.where(even8, o, e), 7, 0)
 
     def lines(a):
         ones = jnp.ones((8, W), jnp.float32)
@@ -349,13 +335,10 @@
         out_e[pl.ds(0, 1), :] = edge_sum(1)
         rep_copy(0, True).wait_recv()
         rep_copy(1, True).wait_recv()
-        unpack(1, 0)
 
     @pl.when(jnp.logical_not(has_low))
     def _():
         put(0, source(0))
-
-    write(0).start()
 
     @pl.when(has_up)
     def _():
@@ -364,19 +347,15 @@
         out_e[pl.ds(R - 1, 1), :] = edge_sum(0)
         rep_copy(0, False).wait_recv()
         rep_copy(1, False).wait_recv()
-        unpack(0, R - 1)
 
     @pl.when(jnp.logical_not(has_up))
     def _():
         put(R - 1, source(R - 1))
-
-    write(R - 1).start()
 
     def drain(r, carry):
         for p in range(2):
             for k in range(4):
                 halo(p, k, r).wait_send()
-        write(r).wait()
         return carry
 
     lax.fori_loop(0, R, drain, 0)
@@ -389,6 +368,45 @@
 
     pl.when(has_up)(lambda: sent(True))
     pl.when(has_low)(lambda: sent(False))
+
+
+def store(sizes, kept, arrived, lines, out, out_e, edge, sem):
+    R, C, T, L = kept.shape
+    ri, ti, si = lax.axis_index("rep"), lax.axis_index("tm"), lax.axis_index("space")
+    lane = lax.broadcasted_iota(jnp.int32, (8, W), 1)
+    sub = lax.broadcasted_iota(jnp.int32, (8, W), 0)
+    even = (lane // LY + lane % LY + sub + si * (L // LY) + ti * T) % 2 == 0
+
+    def from_kept(r):
+        return pltpu.make_async_copy(kept.at[r], out.at[r], sem.at[r])
+
+    def from_edge(u, r):
+        return pltpu.make_async_copy(edge.at[u], out.at[r], sem.at[r])
+
+    for r in range(1, R - 1):
+        from_kept(r).start()
+
+    for u, r, met in ((1, 0, ri > 0), (0, R - 1, ri < sizes[0] - 1)):
+
+        @pl.when(met)
+        def _(u=u, r=r):
+            for c in range(C):
+                for j in range(L // W):
+                    at = pl.ds(j * W, W)
+                    for b in range(T // 16):
+                        e = arrived[u, 0, c, pl.ds(8 * b, 8), at]
+                        o = arrived[u, 1, c, pl.ds(8 * b, 8), at]
+                        edge[u, c, pl.ds(16 * b, 8), at] = jnp.where(even, e, o)
+                        edge[u, c, pl.ds(16 * b + 8, 8), at] = pltpu.roll(jnp.where(even, o, e), 7, 0)
+            from_edge(u, r).start()
+
+        @pl.when(jnp.logical_not(met))
+        def _(r=r):
+            from_kept(r).start()
+
+    out_e[...] = lines[...]
+    for r in range(R):
+        from_kept(r).wait()
 
 
 def on_device(sizes, spins, bond_right, bond_down, betas, time_coupling, thresholds, partner, accept):
@@ -397,26 +415,25 @@
     f32 = jnp.float32
     vm, sm, any_ = (pl.BlockSpec(memory_space=m) for m in (pltpu.VMEM, pltpu.SMEM, pl.ANY))
     dma = pltpu.SemaphoreType.DMA
-    return pl.pallas_call(
+    kept, arrived, lines = pl.pallas_call(
         functools.partial(kernel, sizes),
         out_shape=(
-            jax.ShapeDtypeStruct((R, C, T, L), f32),
-            jax.ShapeDtypeStruct((R, T), f32),
+            pltpu.VMEM((R, C, T, L), f32),
+            pltpu.VMEM((2, 2, C, T // 2, L), f32),
+            pltpu.VMEM((R, T), f32),
         ),
         in_specs=[sm, sm, sm, sm, vm, vm, any_, any_],
-        out_specs=(any_, vm),
+        out_specs=(vm, vm, vm),
         scratch_shapes=[
             pltpu.VMEM((R, C, T, L), f32),
             pltpu.VMEM((R, C, T, L), f32),
             pltpu.VMEM((2, R, T, L), jnp.int32),
-            pltpu.VMEM((R, C, T, L), f32),
             pltpu.VMEM((2, 2, R, C, T, W), f32),
             pltpu.VMEM((2, 2, R, C, 1, L), f32),
             pltpu.VMEM((2, 2, R, C, 1, L), f32),
             pltpu.VMEM((4, 8, L), f32),
             pltpu.VMEM((8, W), f32),
             pltpu.VMEM((8, W), f32),
-            pltpu.VMEM((2, 2, C, T // 2, L), f32),
             pltpu.VMEM((2, 2, C, T // 2, L), f32),
             pltpu.VMEM((nsp, R, T, W), f32),
             pltpu.VMEM((2, nsp, T, W), f32),
@@ -431,13 +448,24 @@
             dma((nsp, R)),
             dma((2, nsp)),
             dma((2, nsp)),
-            dma((R,)),
         ],
         compiler_params=pltpu.CompilerParams(
             collective_id=0, has_side_effects=True, vmem_limit_bytes=56 * 1024 * 1024
         ),
         name="sweep_exchange",
     )(betas, time_coupling, partner, accept, bond_right, bond_down, spins, thresholds)
+    return pl.pallas_call(
+        functools.partial(store, sizes),
+        out_shape=(
+            jax.ShapeDtypeStruct((R, C, T, L), f32),
+            jax.ShapeDtypeStruct((R, T), f32),
+        ),
+        in_specs=[vm, vm, vm],
+        out_specs=(any_, vm),
+        scratch_shapes=[pltpu.VMEM((2, C, T, L), f32), dma((R,))],
+        compiler_params=pltpu.CompilerParams(vmem_limit_bytes=16 * 1024 * 1024),
+        name="store_swapped",
+    )(kept, arrived, lines)
 
 
 def solution(mesh):

time: 28.2 us -> 25.1 us (0.89)
  local copies, waits for them, and re-layouts: 3.62 us -> 0 us
  Pallas kernels: 23.7 us -> 24.3 us
    unnamed x4 -> x0, local copies, waits for them, and re-layouts: 3.62 us -> none
    pallas_call x1 -> x2, Pallas kernels: 23.7 us -> 24.3 us  [the longest x1 22.4 us: on_device(): pl.pallas_call(functools.partial(kernel, sizes), out_shape=(pltpu.VMEM((R...]
where the time goes in v2:
time: 25.1 us; the launch traced here: 24.9 us
  Pallas kernels  24.3 us (97%)
  between operations  0.64 us (3%)
    pallas_call x1, Pallas kernels, on_device(): pl.pallas_call(functools.partial(kernel, sizes), out_shape=(pltpu.VMEM((R...  22.4 us
    pallas_call x1, Pallas kernels, on_device(): pl.pallas_call(functools.partial(store, sizes), out_shape=(jax.ShapeDtype...  1.9 us

profile of v2, /device:TPU:0, one launch (start us, length us, event | category | flops | bytes accessed | tf_op | source)
XLA Modules:
  0.0 24.9 jit_solution(5924859217222157100)
XLA Ops:
  0.6 22.4 %sweep_exchange.1 = (f32[5,3,16,2048]{3,2,1,0:T(8,128)S(1)}, f32[2,2,3,8,2048]{4,3,2,1,0:T(8,128)S(1)}, f32[5,16]{1,0:T(8,128)S(1)}) custom-call(f32[5]{0:T(128)} %betas.1, f32[5]{0:T(128)} %tcs.1, s32[5]{0:T(128)} %partner.1, s32[5]{0:T(128)} %accept.1, f32[2048]{0:T(1024)} %bond_right.1, f32[2048]{0:T(1024)} %bond_down.1, f32[5,3,16,2048]{3,2,1,0:T(8,128)} %spins.1, ...), custom_call_target="tpu_custom_call" | custom-call | tf_op jit(solution)/shard_map/sweep_exchange/pallas_call | solution.py:418
  23.0 1.9 %store_swapped.1 = (f32[5,3,16,2048]{3,2,1,0:T(8,128)}, f32[5,16]{1,0:T(8,128)}) custom-call(f32[5,3,16,2048]{3,2,1,0:T(8,128)S(1)} %get-tuple-element.5.kept, f32[2,2,3,8,2048]{4,3,2,1,0:T(8,128)S(1)} %get-tuple-element.6.arrived, f32[5,16]{1,0:T(8,128)S(1)} %get-tuple-element.7.lines), custom_call_target="tpu_custom_call" | custom-call | tf_op jit(solution)/shard_map/store_swapped/pallas_call | solution.py:457

commit v3 on v2

--- a/solution.py
+++ b/solution.py
@@ -126,38 +126,44 @@
         return jnp.broadcast_to(ref[pl.ds(j * W, W)].reshape(1, W), (8, W))
 
     BDS[...] = row(bond_down, NJ - 1)
-    count = 2 + (nsp - 1) + nsp * (has_low.astype(jnp.int32) + has_up.astype(jnp.int32))
-    pl.semaphore_wait(barrier, count)
-
-    bond_copy.start()
-    for i in range(R):
-        for k in (2, 3):
-            halo(0, k, (i + R - 1) % R).start()
-
     def edges(i, carry):
         r = order(i)
         loads(r)[0].wait()
         for c in range(C):
-            ET[0, 0, r, c] = S[r, c, 0:1, :]
-            ET[0, 1, r, c] = S[r, c, T - 1 : T, :]
+            for j in range(NJ):
+                ET[0, 0, r, c, pl.ds(j, 1), :] = S[r, c, 0:1, pl.ds(j * W, W)]
+                ET[0, 1, r, c, pl.ds(j, 1), :] = S[r, c, T - 1 : T, pl.ds(j * W, W)]
         halo(0, 0, r).start()
         halo(0, 1, r).start()
         return carry
 
-    lax.fori_loop(0, R, edges, 0)
-
-    bond_copy.wait()
-    prev_rot = pltpu.roll(BDH[...], LY, 1)
+    def edges_out(i, carry):
+        r = order(i)
+        for k in (2, 3):
+            halo(0, k, r).start()
+        return carry
+
+    prev_rot = None
     for j in range(NJ):
         bd = row(bond_down, j)
         br = row(bond_right, j)
         rot = pltpu.roll(bd, LY, 1)
         BO[0, :, pl.ds(j * W, W)] = bd
-        BO[1, :, pl.ds(j * W, W)] = jnp.where(lo8, prev_rot, rot)
+        BO[1, :, pl.ds(j * W, W)] = rot if j == 0 else jnp.where(lo8, prev_rot, rot)
         BO[2, :, pl.ds(j * W, W)] = br
         rot_r = pltpu.roll(br, LY, 1)
         BO[3, :, pl.ds(j * W, W)] = pltpu.roll(jnp.where(lane % LY == LY - 1, rot_r, br), 1, 1)
         prev_rot = rot
+
+    count = 2 + (nsp - 1) + nsp * (has_low.astype(jnp.int32) + has_up.astype(jnp.int32))
+    pl.semaphore_wait(barrier, count)
+
+    bond_copy.start()
+    lax.fori_loop(0, R, edges_out, 0)
+    lax.fori_loop(0, R, edges, 0)
+
+    bond_copy.wait()
+    BO[1, :, pl.ds(0, W)] = jnp.where(lo8, pltpu.roll(BDH[...], LY, 1), BO[1, :, pl.ds(0, W)])
 
     def tall(x):
         return jnp.concatenate([x] * (T // 8), axis=0)
@@ -191,8 +197,8 @@
                 right = pltpu.roll(jnp.where(col0, here[c], s), W - 1, 1)
                 left = pltpu.roll(jnp.where(col_last, here[c], s), 1, 1)
                 fs = bd * down + bu * up + br * right + bl * left
-                later = jnp.where(t_last, HT[p, 1, r, c, :, at], pltpu.roll(s, T - 1, 0))
-                earlier = jnp.where(t_first, HT[p, 0, r, c, :, at], pltpu.roll(s, 1, 0))
+                later = jnp.where(t_last, HT[p, 1, r, c, pl.ds(j, 1), :], pltpu.roll(s, T - 1, 0))
+                earlier = jnp.where(t_first, HT[p, 0, r, c, pl.ds(j, 1), :], pltpu.roll(s, 1, 0))
                 field = beta * fs + tc * (later + earlier)
                 old.append(s)
                 fields.append(fs)
@@ -204,8 +210,8 @@
                 if p == 0:
                     new = jnp.where(even, fresh, old[c])
                     S[r, c, :, at] = new
-                    ET[1, 0, r, c, :, at] = new[0:1]
-                    ET[1, 1, r, c, :, at] = new[T - 1 : T]
+                    ET[1, 0, r, c, pl.ds(j, 1), :] = new[0:1]
+                    ET[1, 1, r, c, pl.ds(j, 1), :] = new[T - 1 : T]
                 else:
                     new = jnp.where(even, old[c], fresh)
                     F[r, c, :, at] = new
@@ -429,8 +435,8 @@
             pltpu.VMEM((R, C, T, L), f32),
             pltpu.VMEM((2, R, T, L), jnp.int32),
             pltpu.VMEM((2, 2, R, C, T, W), f32),
-            pltpu.VMEM((2, 2, R, C, 1, L), f32),
-            pltpu.VMEM((2, 2, R, C, 1, L), f32),
+            pltpu.VMEM((2, 2, R, C, L // W, W), f32),
+            pltpu.VMEM((2, 2, R, C, L // W, W), f32),
             pltpu.VMEM((4, 8, L), f32),
             pltpu.VMEM((8, W), f32),
             pltpu.VMEM((8, W), f32),

time: 25.1 us -> 25.1 us (level)
  no operation moved by 1% of the time
where the time goes in v3:
time: 25.1 us; the launch traced here: 24.9 us
  Pallas kernels  24.3 us (97%)
  between operations  0.64 us (3%)
    pallas_call x1, Pallas kernels, on_device(): pl.pallas_call(functools.partial(kernel, sizes), out_shape=(pltpu.VMEM((R...  22.4 us
    pallas_call x1, Pallas kernels, on_device(): pl.pallas_call(functools.partial(store, sizes), out_shape=(jax.ShapeDtype...  1.9 us

profile of v3, /device:TPU:0, one launch (start us, length us, event | category | flops | bytes accessed | tf_op | source)
XLA Modules:
  0.0 24.9 jit_solution(13141688940070345722)
XLA Ops:
  0.6 22.4 %sweep_exchange.1 = (f32[5,3,16,2048]{3,2,1,0:T(8,128)S(1)}, f32[2,2,3,8,2048]{4,3,2,1,0:T(8,128)S(1)}, f32[5,16]{1,0:T(8,128)S(1)}) custom-call(f32[5]{0:T(128)} %betas.1, f32[5]{0:T(128)} %tcs.1, s32[5]{0:T(128)} %partner.1, s32[5]{0:T(128)} %accept.1, f32[2048]{0:T(1024)} %bond_right.1, f32[2048]{0:T(1024)} %bond_down.1, f32[5,3,16,2048]{3,2,1,0:T(8,128)} %spins.1, ...), custom_call_target="tpu_custom_call" | custom-call | tf_op jit(solution)/shard_map/sweep_exchange/pallas_call | solution.py:424
  23.0 1.9 %store_swapped.1 = (f32[5,3,16,2048]{3,2,1,0:T(8,128)}, f32[5,16]{1,0:T(8,128)}) custom-call(f32[5,3,16,2048]{3,2,1,0:T(8,128)S(1)} %get-tuple-element.5.kept, f32[2,2,3,8,2048]{4,3,2,1,0:T(8,128)S(1)} %get-tuple-element.6.arrived, f32[5,16]{1,0:T(8,128)S(1)} %get-tuple-element.7.lines), custom_call_target="tpu_custom_call" | custom-call | tf_op jit(solution)/shard_map/store_swapped/pallas_call | solution.py:463
